TPU v7x, 32 devices: a whole 2x2x4 slice. The times are simulated.
32 devices in a mesh: dp: 8 (over z, y), mp: 4 (over x, core).
Axes of the slice: x: 2, y: 2, z: 4, core: 2. Of those that a mesh axis runs over, the one named last changes fastest.
Arguments:
- queries: bfloat16 [24576, 2048], P('dp', 'mp'), may hold values from -30 to 30
- keys: bfloat16 [24576, 512], P('dp', 'mp'), may hold values from -30 to 30
- values: bfloat16 [24576, 512], P('dp', 'mp'), may hold values from -6 to 6
- doc_ids: int32 [24576], P('dp'), may hold values from -1 to 127, as said below
- live_counts: int32 [8], P('dp'), may hold values from 1 to 24, 176 in all
- out_weight: bfloat16 [2048, 4096], P('dp', 'mp'), may hold values from -0.125 to 0.125
Outputs:
- mixed: bfloat16 [22528, 4096], P('dp', 'mp')
Inputs may be any that keep to these rules, and one draw needn't show every extreme that they name: `live_counts`: each device has 1 to 24 live blocks, 176 in all, and some device has exactly 24. `doc_ids`: within each block the numbers start at 0 and never fall along the block, and the -1 entries, if any, form the block's tail.
All inputs are finite; a program needn't handle non-finite values.
Results may differ from a plain program's by a relative error of at most 0.0049.
Values may be sent and summed in bfloat16 or wider, within the bound.
A program may use at most 128 MiB of HBM per device.

v0:
```python
import math

import jax
import jax.numpy as jnp
from jax import lax
from jax.sharding import PartitionSpec as P

HEAD_SIZE = 128
BLOCK = 128
NB = 24


masked_score = -1e30


def group_size():
    return 4


def attend_group(operands):
    query_blocks, key_blocks, value_blocks, id_blocks = operands
    number = query_blocks.shape[0]
    query_heads = query_blocks.shape[2] // HEAD_SIZE
    key_heads = key_blocks.shape[2] // HEAD_SIZE
    repeat = query_heads // key_heads
    query_four = query_blocks.reshape(number, BLOCK, key_heads, repeat, HEAD_SIZE)
    key_four = key_blocks.reshape(number, BLOCK, key_heads, HEAD_SIZE)
    value_four = value_blocks.reshape(number, BLOCK, key_heads, HEAD_SIZE)
    scores = jnp.einsum(
        "bihrd,bjhd->bhrij", query_four, key_four, preferred_element_type=jnp.float32
    ) / math.sqrt(HEAD_SIZE)
    places = jnp.arange(BLOCK, dtype=jnp.int32)
    causal = places[None, :] <= places[:, None]
    allowed = (id_blocks[:, :, None] == id_blocks[:, None, :]) & causal[None]
    scores = jnp.where(allowed[:, None, None], scores, masked_score)
    highest = jnp.max(scores, axis=-1, keepdims=True)
    weights = jnp.where(allowed[:, None, None], jnp.exp(scores - highest), 0.0)
    total_counts = jnp.sum(weights, axis=-1)
    summed = jnp.einsum(
        "bhrij,bjhd->bihrd",
        weights.astype(jnp.bfloat16),
        value_four,
        preferred_element_type=jnp.float32,
    )
    summed = summed / jnp.transpose(total_counts, (0, 3, 1, 2))[..., None]
    summed = jnp.where(id_blocks[:, :, None, None, None] >= 0, summed, 0.0)
    return summed.reshape(number, BLOCK, query_heads * HEAD_SIZE).astype(jnp.bfloat16)


def attend_blocks(query_blocks, key_blocks, value_blocks, id_blocks):
    number = query_blocks.shape[0]
    grouping = group_size()

    def regroup(tensor):
        return tensor.reshape((number // grouping, grouping) + tensor.shape[1:])

    result = lax.map(
        attend_group,
        (regroup(query_blocks), regroup(key_blocks), regroup(value_blocks), regroup(id_blocks)),
    )
    return result.reshape((number,) + result.shape[2:])


def locate(labels, targets):
    slots = jnp.arange(labels.shape[0], dtype=jnp.int32)
    hits = labels[None, :] == targets[:, None]
    return jnp.sum(jnp.where(hits, slots[None, :], 0), axis=1)


def body(queries, keys, values, doc_ids, live_counts, out_weight):
    member_list = lax.axis_size("dp")
    per_owner = (NB + member_list - 1) // member_list
    kept_blocks = NB * 11 // 12
    own_index = lax.axis_index("dp")
    live_blocks = live_counts[0]
    full_weight = lax.all_gather(out_weight, "dp", axis=0, tiled=True)
    table = lax.all_gather(live_counts, "dp", axis=0, tiled=True)
    first_label = jnp.sum(jnp.where(jnp.arange(member_list, dtype=jnp.int32) < own_index, table, 0))
    owners = jnp.arange(member_list, dtype=jnp.int32)[:, None]
    layers = jnp.arange(per_owner, dtype=jnp.int32)[None, :]
    chosen = ((owners - first_label) % member_list + layers * member_list).reshape(-1)
    usable = chosen < live_blocks
    labels = jnp.where(usable, first_label + chosen, -1)
    chosen = jnp.where(usable, chosen, 0)
    query_cols = queries.shape[1]
    query_blocks = queries.reshape(NB, BLOCK, query_cols)
    key_blocks = keys.reshape(NB, BLOCK, keys.shape[1])
    value_blocks = values.reshape(NB, BLOCK, values.shape[1])
    id_blocks = doc_ids.reshape(NB, BLOCK)
    targets = own_index + jnp.arange(kept_blocks, dtype=jnp.int32) * member_list
    own_result = attend_blocks(query_blocks, key_blocks, value_blocks, id_blocks)
    arrived = (
        lax.all_to_all(own_result[chosen], "dp", split_axis=0, concat_axis=0, tiled=True),
        lax.all_to_all(labels, "dp", split_axis=0, concat_axis=0, tiled=True),
    )
    source = locate(arrived[1], targets)
    attended = arrived[0][source]
    flattened = attended.reshape(kept_blocks * BLOCK, query_cols)
    mixed = jnp.dot(
        lax.all_gather(flattened, "mp", axis=1, tiled=True),
        full_weight,
        preferred_element_type=jnp.float32,
    )
    return mixed.astype(jnp.bfloat16)


def solution(mesh):
    return jax.shard_map(
        body,
        mesh=mesh,
        in_specs=(P("dp", "mp"), P("dp", "mp"), P("dp", "mp"), P("dp"), P("dp"), P("dp", "mp")),
        out_specs=P("dp", "mp"),
        check_vma=False,
    )
```

profile of v0, /device:TPU:1, one launch (start us, length us, event | category | flops | bytes accessed | tf_op | source)
XLA Modules:
  0.0 253.6 jit_solution(2867738865714764255)
XLA Ops:
  7.9 1.2 dynamic-slice
  9.9 9.5 %all-reduce = s32[8]{0:T(128)S(1)} all-reduce(s32[8]{0:T(128)S(1)} %dynamic-update-slice), channel_id=1, replica_groups=mesh['dp'=8,'mp'=4] {'dp'}, use_global_device_ids=true, to_apply=%add | all-reduce | flops 8 | bytes 64
  20.8 1.3 compare_select_fusion
  22.1 3.2 %all-to-all-start.1 = ((s32[8,3,1]{1,2,0:T(1,128)}), s32[8,3,1]{1,2,0:T(1,128)S(1)}, u32[]{:S(2)}, u32[]{:S(2)}) async-start(s32[8,3,1]{1,2,0:T(1,128)} %compare_select_fusion), calls=%async_computation.1 | async-start | bytes 8192 | tf_op jit(solution)/shard_map/all_to_all | solution.py:94
  25.3 35.9 %while.10 = (s32[]{:T(128)}, bf16[6,4,128,512]{3,2,1,0:T(8,128)(2,1)}, s32[6,4,128]{2,1,0:T(4,128)}, bf16[6,4,128,128]{3,2,1,0:T(8,128)(2,1)}, bf16[6,4,128,128]...) while((s32[]{:T(128)}, bf16[6,4,128,512]{3,2,1,0:T(8,128)(2,1)}, s32[6,4,128]{2,1,0:T(4,128)}, ...), condition=%wide.region_3.4_spmd, body=%wide.region_0.3_spmd.sunk | while | flops 137507328 | bytes 8993897 | solution.py:57
  26.2 1.1 constant_dynamic-slice_fusion.2
  27.6 1.2 fusion.32
  29.0 1.3 select_convert_fusion.2
  30.5 0.8 constant_dynamic-update-slice_fusion.2
  32.2 1.1 constant_dynamic-slice_fusion.2
  33.5 1.2 fusion.32
  35.0 1.3 select_convert_fusion.2
  36.4 0.8 constant_dynamic-update-slice_fusion.2
  38.1 1.1 constant_dynamic-slice_fusion.2
  39.5 1.2 fusion.32
  40.9 1.3 select_convert_fusion.2
  42.4 0.8 constant_dynamic-update-slice_fusion.2
  44.1 1.1 constant_dynamic-slice_fusion.2
  45.4 1.3 fusion.32
  46.9 1.3 select_convert_fusion.2
  50.1 1.1 constant_dynamic-slice_fusion.2
  51.5 1.2 fusion.32
  52.9 1.3 select_convert_fusion.2
  56.1 1.1 constant_dynamic-slice_fusion.2
  57.4 1.2 fusion.32
  58.9 1.3 select_convert_fusion.2
  61.3 4.4 %gather_fusion = bf16[24,128,512]{2,1,0:T(8,128)(2,1)} fusion(bf16[24,128,512]{2,1,0:T(8,128)(2,1)} %bitcast.79, s32[1024]{0:T(1024)S(1)} %pad_clamp_fusion.1), kind=kCustom, calls=%fused_computation | custom fusion | bytes 6291552 | tf_op jit(solution)/shard_map/gather | solution.py:93
  65.8 5.3 %all-to-all-start = ((bf16[24,128,512]{2,1,0:T(8,128)(2,1)}), bf16[24,128,512]{2,1,0:T(8,128)(2,1)S(1)}, u32[]{:S(2)}, u32[]{:S(2)}) async-start(bf16[24,128,512]{2,1,0:T(8,128)(2,1)} %gather_fusion), calls=%async_computation | async-start | bytes 6291456 | tf_op jit(solution)/shard_map/all_to_all | solution.py:93
  72.6 78.4 %all-to-all-done = bf16[24,128,512]{2,1,0:T(8,128)(2,1)S(1)} async-done(((bf16[24,128,512]{2,1,0:T(8,128)(2,1)}), bf16[24,128,512]{2,1,0:T(8,128)(2,1)S(1)}, u32[]{:S(2)}, u32[]{:S(2)}) %all-to-all-start) | async-done | bytes 3145760 | tf_op jit(solution)/shard_map/all_to_all | solution.py:93
  151.0 2.4 gather_fusion.1
  153.5 75.4 %all-gather.3.cloned.1.call-done = bf16[2816,2048]{1,0:T(8,128)(2,1)} async-done(((bf16[2816,512]{1,0:T(8,128)(2,1)}), bf16[2816,2048]{1,0:T(8,128)(2,1)}) %all-gather.3.cloned.1.call-update) | async-done | bytes 11534352 | tf_op jit(solution)/shard_map/all_gather | solution.py:100
  229.0 17.8 %convolution_convert_fusion = bf16[2816,1024]{1,0:T(8,128)(2,1)} fusion(bf16[2816,2048]{1,0:T(8,128)(2,1)} %all-gather.3.cloned.1.call-done, bf16[2048,1024]{1,0:T(8,128)(2,1)} %all-gather.5.cloned.1.call-done), kind=kOutput, calls=%fused_computation.27 | convolution fusion | flops 11814043648 | bytes 21495808 | tf_op jit(solution)/shard_map/dot_general | solution.py:99
  (62 shorter events, 16.2 us)
Async XLA Ops:
  6.5 147.0 %all-gather.5.cloned.1.call-start = ((), (), s32[]{:S(2)}) async-start(), calls=%async_computation.3 | async-start | bytes 4718592 | tf_op jit(solution)/shard_map/all_gather | solution.py:76
  22.1 43.7 %all-to-all-start.1 = ((s32[8,3,1]{1,2,0:T(1,128)}), s32[8,3,1]{1,2,0:T(1,128)S(1)}, u32[]{:S(2)}, u32[]{:S(2)}) async-start(s32[8,3,1]{1,2,0:T(1,128)} %compare_select_fusion), calls=%async_computation.1 | async-start | bytes 8192 | tf_op jit(solution)/shard_map/all_to_all | solution.py:94
  65.8 85.3 %all-to-all-start = ((bf16[24,128,512]{2,1,0:T(8,128)(2,1)}), bf16[24,128,512]{2,1,0:T(8,128)(2,1)S(1)}, u32[]{:S(2)}, u32[]{:S(2)}) async-start(bf16[24,128,512]{2,1,0:T(8,128)(2,1)} %gather_fusion), calls=%async_computation | async-start | bytes 6291456 | tf_op jit(solution)/shard_map/all_to_all | solution.py:93
  71.1 157.9 %all-gather.3.cloned.1.call-start = ((), (), s32[]{:S(2)}) async-start(), calls=%async_computation.2 | async-start | bytes 14417920 | tf_op jit(solution)/shard_map/all_gather | solution.py:100
Sparse Core Ops, SparseCore 0:
  9.5 79.1 all-gather.4
  153.6 75.3 all-gather.2
where the time goes:
time: 255 us; the launch traced here: 254 us
  waiting for transfers between devices  155 us (61%)
  matrix products  32.6 us (13%)
  local copies, waits for them, and re-layouts  23.9 us (9%)
  between operations  14.1 us (6%)
  other arithmetic  9.88 us (4%)
  blocking collectives  9.54 us (4%)
  starting transfers between devices  8.6 us (3%)
    all_to_all x1, waiting for transfers between devices, body(): lax.all_to_all(own_result[chosen], 'dp', split_axis=0, concat_axis=0, til...  78.4 us
    all_gather x1, waiting for transfers between devices, body(): lax.all_gather(flattened, 'mp', axis=1, tiled=True)  75.4 us
    dot_general x1, matrix products, body(): jnp.dot(lax.all_gather(flattened, 'mp', axis=1, tiled=True), full_weight,...  17.8 us
    unnamed x1, blocking collectives  9.54 us
    dynamic_slice x12, local copies, waits for them, and re-layouts, attend_blocks(): lax.map(attend_group, (regroup(query_blocks), regroup(key_blocks), regrou...  8.12 us
    dot_general x6, matrix products, attend_group(): jnp.einsum('bhrij,bjhd->bihrd', weights.astype(jnp.bfloat16), value_four,...  7.53 us
    dot_general x6, matrix products, attend_group(): jnp.einsum('bihrd,bjhd->bhrij', query_four, key_four, preferred_element_t...  7.35 us
    dynamic_update_slice x12, local copies, waits for them, and re-layouts, attend_blocks(): lax.map(attend_group, (regroup(query_blocks), regroup(key_blocks), regrou...  6.28 us
  transfers between devices with their start and end apart: 4, of which 2 were waited for; matrix products, arithmetic and copies ran while one was open for 19% of the time, Pallas kernels for 0%

commit v1 on v0

v1 whole, which is shorter than its diff:
```python
import functools
import math

import jax
import jax.numpy as jnp
from jax import lax
from jax.experimental import pallas as pl
from jax.experimental.pallas import tpu as pltpu
from jax.sharding import PartitionSpec as P

HEAD_SIZE = 128
BLOCK = 128
NB = 24
MESH = pl.DeviceIdType.MESH
MASKED = -1e30


def attend_kernel(per_owner, chosen_ref, queries_ref, keys_ref, values_ref, ids_ref, out_ref):
    step = pl.program_id(0)
    repeat = queries_ref.shape[1] // HEAD_SIZE
    factor = math.log2(math.e) / math.sqrt(HEAD_SIZE)
    row_at = lax.broadcasted_iota(jnp.int32, (BLOCK, BLOCK), 0)
    col_at = lax.broadcasted_iota(jnp.int32, (BLOCK, BLOCK), 1)
    causal = col_at <= row_at
    for layer in range(per_owner):
        block = chosen_ref[step * per_owner + layer]
        rows = pl.ds(pl.multiple_of(block * BLOCK, BLOCK), BLOCK)
        along = jnp.broadcast_to(ids_ref[pl.ds(block, 1), :], (BLOCK, BLOCK))
        down = along.T
        allowed = (along == down) & causal
        real = down >= 0
        key = keys_ref[rows, :]
        value = values_ref[rows, :]
        for head in range(repeat):
            columns = slice(head * HEAD_SIZE, (head + 1) * HEAD_SIZE)
            query = queries_ref[rows, columns]
            scores = lax.dot_general(
                query, key, (((1,), (1,)), ((), ())), preferred_element_type=jnp.float32
            )
            scores = jnp.where(allowed, scores, MASKED)
            highest = jnp.max(scores, axis=1, keepdims=True)
            weights = jnp.exp2((scores - highest) * factor)
            totals = jnp.sum(weights, axis=1, keepdims=True)
            summed = jnp.dot(
                weights.astype(jnp.bfloat16), value, preferred_element_type=jnp.float32
            )
            summed = jnp.where(real, summed / totals, 0.0)
            out_ref[0, layer, :, columns] = summed.astype(out_ref.dtype)


def attend(chosen, queries, keys, values, ids, members, per_owner):
    cols = queries.shape[1]

    def whole(array):
        return pl.BlockSpec(array.shape, lambda i, c: (0, 0))

    return pl.pallas_call(
        functools.partial(attend_kernel, per_owner),
        out_shape=jax.ShapeDtypeStruct((members, per_owner, BLOCK, cols), jnp.bfloat16),
        grid_spec=pltpu.PrefetchScalarGridSpec(
            num_scalar_prefetch=1,
            grid=(members,),
            in_specs=[whole(queries), whole(keys), whole(values), whole(ids)],
            out_specs=pl.BlockSpec((1, per_owner, BLOCK, cols), lambda i, c: (i, 0, 0, 0)),
        ),
        compiler_params=pltpu.CompilerParams(vmem_limit_bytes=40 * 1024 * 1024),
        cost_estimate=pl.CostEstimate(
            flops=members * per_owner * cols * BLOCK * BLOCK * 4,
            bytes_accessed=4 * queries.size,
            transcendentals=members * per_owner * cols * BLOCK,
        ),
    )(chosen, queries, keys, values, ids)


def flip(index, mask):
    bit = 1
    while bit <= mask:
        if mask & bit:
            index = index + bit - 2 * bit * ((index // bit) % 2)
        bit *= 2
    return index


def exchange_kernel(
    members, columns, per_owner,
    sent_ref, weight_ref, far_weight_ref, held_ref, full_ref,
    local_sem, send_dp, recv_dp, send_x, recv_x, send_w, recv_w,
):
    me = lax.axis_index("dp")
    mine = lax.axis_index("mp")
    top = members // 2

    def dp_device(mask):
        return (flip(me, mask), mine)

    def mp_device(mask):
        return (me, flip(mine, mask))

    bits = [1 << b for b in reversed(range(columns.bit_length() - 1))]
    barrier = pltpu.get_barrier_semaphore()
    for mask in range(1, members):
        pl.semaphore_signal(barrier, inc=1, device_id=dp_device(mask), device_id_type=MESH)
    for mask in bits:
        pl.semaphore_signal(barrier, inc=1, device_id=mp_device(mask), device_id_type=MESH)
    pl.semaphore_wait(barrier, members - 1 + len(bits))

    def dp_copy(mask, layer, source):
        return pltpu.make_async_remote_copy(
            src_ref=sent_ref.at[flip(me, mask), layer],
            dst_ref=held_ref.at[mine, source, layer],
            send_sem=send_dp.at[mask, layer],
            recv_sem=recv_dp.at[mask, layer],
            device_id=dp_device(mask),
            device_id_type=MESH,
        )

    def mp_copy(place, bit, mask, layer):
        source = flip(me, mask)
        column = flip(mine, place)
        if mask == 0 and place == 0:
            src = sent_ref.at[source, layer]
        else:
            src = held_ref.at[column, source, layer]
        return pltpu.make_async_remote_copy(
            src_ref=src,
            dst_ref=held_ref.at[column, source, layer],
            send_sem=send_x.at[place ^ bit, mask, layer],
            recv_sem=recv_x.at[place ^ bit, mask, layer],
            device_id=mp_device(bit),
            device_id_type=MESH,
        )

    def weight_copy(mask, bit):
        owner = flip(me, mask)
        if mask == 0:
            src = weight_ref
        elif mask == top:
            src = far_weight_ref
        else:
            src = full_ref.at[owner]
        return pltpu.make_async_remote_copy(
            src_ref=src,
            dst_ref=full_ref.at[owner],
            send_sem=send_w.at[mask ^ bit],
            recv_sem=recv_w.at[mask ^ bit],
            device_id=dp_device(bit),
            device_id_type=MESH,
        )

    local = [
        pltpu.make_async_copy(weight_ref, full_ref.at[me], local_sem.at[0]),
        pltpu.make_async_copy(far_weight_ref, full_ref.at[flip(me, top)], local_sem.at[1]),
        pltpu.make_async_copy(sent_ref.at[me], held_ref.at[mine, me], local_sem.at[2]),
    ]
    started = []

    def start(copy):
        copy.start()
        started.append(copy)

    def spread_weight(mask, below):
        bit = below // 2
        while bit >= 1:
            start(weight_copy(mask, bit))
            bit //= 2

    def spread(place, below, mask, layer):
        for bit in bits:
            if bit < below:
                start(mp_copy(place, bit, mask, layer))

    order = sorted(range(1, members), key=lambda t: (-(bin(t).count("1") % 2), t))
    spread_weight(0, top)
    spread_weight(top, top)
    for layer in range(per_owner):
        spread(0, columns, 0, layer)
        for mask in order:
            start(dp_copy(mask, layer, me))
    for copy in local:
        copy.start()

    chunks = [(0, layer) for layer in range(per_owner)]
    chunks += [(mask, layer) for layer in range(per_owner) for mask in order]
    weights = [t for t in range(1, members) if t != top]
    weights.sort(key=lambda t: (-(t & -t), t))
    lag = 3

    def relay(mask, layer):
        for place in range(1, columns):
            lowest = place & -place
            mp_copy(place ^ lowest, lowest, mask, layer).wait_recv()
            spread(place, lowest, mask, layer)

    for at in range(len(chunks) + lag):
        if at < len(chunks):
            mask, layer = chunks[at]
            if mask:
                dp_copy(mask, layer, me).wait_recv()
                spread(0, columns, mask, layer)
        if at % 3 == 2 and weights:
            arrived = weights.pop(0)
            lowest = arrived & -arrived
            weight_copy(arrived ^ lowest, lowest).wait_recv()
            spread_weight(arrived, lowest)
        if at >= lag:
            relay(*chunks[at - lag])
    for arrived in weights:
        lowest = arrived & -arrived
        weight_copy(arrived ^ lowest, lowest).wait_recv()
        spread_weight(arrived, lowest)
    for copy in started:
        copy.wait_send()
    for copy in local:
        copy.wait()


def exchange(sent, weight, far_weight, members, columns):
    per_owner = sent.shape[1]
    anywhere = pl.BlockSpec(memory_space=pl.ANY)
    dma = pltpu.SemaphoreType.DMA
    return pl.pallas_call(
        functools.partial(exchange_kernel, members, columns, per_owner),
        out_shape=(
            jax.ShapeDtypeStruct((columns,) + sent.shape, sent.dtype),
            jax.ShapeDtypeStruct((members,) + weight.shape, weight.dtype),
        ),
        in_specs=[anywhere] * 3,
        out_specs=(anywhere, anywhere),
        scratch_shapes=[
            dma((3,)),
            dma((members, per_owner)),
            dma((members, per_owner)),
            dma((columns, members, per_owner)),
            dma((columns, members, per_owner)),
            dma((members,)),
            dma((members,)),
        ],
        compiler_params=pltpu.CompilerParams(collective_id=0, has_side_effects=True),
        cost_estimate=pl.CostEstimate(
            flops=0, bytes_accessed=60 * sent.size, transcendentals=0
        ),
    )(sent, weight, far_weight)


def project_kernel(columns, slots_ref, first_ref, second_ref, weight_ref, out_ref):
    total = None
    for column in range(columns):
        rows = jnp.concatenate([first_ref[column, 0], second_ref[column, 0]], axis=0)
        depth = rows.shape[1]
        part = jnp.dot(
            rows, weight_ref[column * depth:(column + 1) * depth, :],
            preferred_element_type=jnp.float32,
        )
        total = part if total is None else total + part
    out_ref[...] = total.astype(out_ref.dtype)


def project(slots, held, weight, kept):
    columns, total, _, depth = held.shape
    width = weight.shape[1]

    def picked(which):
        return pl.BlockSpec(
            (columns, 1, BLOCK, depth), lambda i, s: (0, s[2 * i + which], 0, 0)
        )

    return pl.pallas_call(
        functools.partial(project_kernel, columns),
        out_shape=jax.ShapeDtypeStruct((kept * BLOCK, width), jnp.bfloat16),
        grid_spec=pltpu.PrefetchScalarGridSpec(
            num_scalar_prefetch=1,
            grid=(kept // 2,),
            in_specs=[
                picked(0),
                picked(1),
                pl.BlockSpec(weight.shape, lambda i, s: (0, 0)),
            ],
            out_specs=pl.BlockSpec((2 * BLOCK, width), lambda i, s: (i, 0)),
        ),
        compiler_params=pltpu.CompilerParams(vmem_limit_bytes=40 * 1024 * 1024),
    )(slots, held, held, weight)


def body(members, columns, queries, keys, values, doc_ids, live_counts, out_weight):
    per_owner = (NB + members - 1) // members
    kept = NB * 11 // 12
    own = lax.axis_index("dp")
    half = members // 2
    far_weight = lax.ppermute(
        out_weight, "dp", [(i, (i + half) % members) for i in range(members)]
    )
    table = lax.all_gather(live_counts, "dp", axis=0, tiled=True)
    places = jnp.arange(members, dtype=jnp.int32)
    before = places[None, :] < places[:, None]
    starts = jnp.sum(jnp.where(before, table[None, :], 0), axis=1)
    first_label = jnp.sum(jnp.where(places < own, table, 0))
    owners = jnp.arange(members, dtype=jnp.int32)[:, None]
    layers = jnp.arange(per_owner, dtype=jnp.int32)[None, :]
    chosen = ((owners - first_label) % members + layers * members).reshape(-1)
    chosen = jnp.minimum(chosen, NB - 1)
    wanted = own + jnp.arange(kept, dtype=jnp.int32) * members
    within = wanted[:, None] - starts[None, :]
    holds = (within >= 0) & (within < table[None, :])
    slots = jnp.sum(
        jnp.where(holds, places[None, :] * per_owner + within // members, 0), axis=1
    )
    sent = attend(
        chosen, queries, keys, values, doc_ids.reshape(NB, BLOCK), members, per_owner
    )
    held, full = exchange(sent, out_weight, far_weight, members, columns)
    held = held.reshape(columns, members * per_owner, BLOCK, queries.shape[1])
    full = full.reshape(members * out_weight.shape[0], out_weight.shape[1])
    return project(slots, held, full, kept)


def solution(mesh):
    return jax.shard_map(
        functools.partial(body, mesh.shape["dp"], mesh.shape["mp"]),
        mesh=mesh,
        in_specs=(P("dp", "mp"), P("dp", "mp"), P("dp", "mp"), P("dp"), P("dp"), P("dp", "mp")),
        out_specs=P("dp", "mp"),
        check_vma=False,
    )
```

time: 255 us -> 200 us (0.78)
  Pallas kernels: 0 us -> 162 us
  waiting for transfers between devices: 155 us -> 0.01 us
  matrix products: 32.6 us -> 0 us
  between operations: 14.1 us -> 0.71 us
  local copies, waits for them, and re-layouts: 23.9 us -> 11.6 us
  blocking collectives: 9.54 us -> 20.6 us
  other arithmetic: 9.88 us -> 1.58 us
  starting transfers between devices: 8.6 us -> 3.13 us
    pallas_call x0 -> x3, Pallas kernels: none -> 162 us  [the longest x1 120 us: exchange(): pl.pallas_call(functools.partial(exchange_kernel, members, columns, per_o...]
    all_to_all x2 -> x0, waiting for transfers between devices: 78.4 us -> none  [the longest x1 78.4 us: body(): lax.all_to_all(own_result[chosen], 'dp', split_axis=0, concat_axis=0, til...]
    all_gather x2 -> x0, waiting for transfers between devices: 75.5 us -> none  [the longest x1 75.4 us: body(): lax.all_gather(flattened, 'mp', axis=1, tiled=True)]
    dot_general x13 -> x0, matrix products: 32.6 us -> none  [the longest x1 17.8 us: body(): jnp.dot(lax.all_gather(flattened, 'mp', axis=1, tiled=True), full_weight,...]
    unnamed x1, blocking collectives: 9.54 us -> 20.6 us
    unnamed x3 -> x17, local copies, waits for them, and re-layouts: 2 us -> 11.5 us
    all_to_all x2 -> x0, starting transfers between devices: 8.56 us -> none  [the longest x1 5.34 us: body(): lax.all_to_all(own_result[chosen], 'dp', split_axis=0, concat_axis=0, til...]
    dynamic_slice x12 -> x0, local copies, waits for them, and re-layouts: 8.12 us -> none  [attend_blocks(): lax.map(attend_group, (regroup(query_blocks), regroup(key_blocks), regrou...]
  transfers between devices with their start and end apart: 4 -> 1, of which waited for: 2 -> 0; matrix products, arithmetic and copies ran while one was open for 19% -> 2% of each run, Pallas kernels for 0% -> 12%
where the time goes in v1:
time: 200 us; the launch traced here: 199 us
  Pallas kernels  162 us (81%)
  blocking collectives  20.6 us (10%)
  local copies, waits for them, and re-layouts  11.6 us (6%)
  starting transfers between devices  3.13 us (2%)
    pallas_call x1, Pallas kernels, exchange(): pl.pallas_call(functools.partial(exchange_kernel, members, columns, per_o...  120 us
    pallas_call x1, Pallas kernels, attend(): pl.pallas_call(functools.partial(attend_kernel, per_owner), out_shape=jax...  24.5 us
    unnamed x1, blocking collectives  20.6 us
    pallas_call x1, Pallas kernels, project(): pl.pallas_call(functools.partial(project_kernel, columns), out_shape=jax....  17.1 us
    unnamed x17, local copies, waits for them, and re-layouts  11.5 us
  transfers between devices with their start and end apart: 1, of which 0 were waited for; matrix products, arithmetic and copies ran while one was open for 2% of the time, Pallas kernels for 12%

profile of v1, /device:TPU:1, one launch (start us, length us, event | category | flops | bytes accessed | tf_op | source)
XLA Modules:
  0.0 199.5 jit_solution(12239338584074783666)
XLA Ops:
  0.0 3.1 %collective-permute-start = (bf16[256,1024]{1,0:T(8,128)(2,1)}, bf16[256,1024]{1,0:T(8,128)(2,1)S(1)}, u32[]{:S(2)}, u32[]{:S(2)}) collective-permute-start(bf16[256,1024]{1,0:T(8,128)(2,1)} %weight_ref.1), channel_id=1, source_target_pairs={{0,16},{4,20},{8,24},{12,28},{16,0},{20,4},{24,8},{28,12},{1,17},{... | collective-permute-start | bytes 1572872 | tf_op jit(solution)/shard_map/ppermute | solution.py:289
  3.8 1.2 dynamic-slice
  5.0 0.8 dynamic-update-slice
  5.8 20.6 %all-reduce = s32[8]{0:T(128)S(1)} all-reduce(s32[8]{0:T(128)S(1)} %dynamic-update-slice), channel_id=1, replica_groups=mesh['dp'=8,'mp'=4] {'dp'}, use_global_device_ids=true, to_apply=%add | all-reduce | flops 8 | bytes 64
  26.4 0.6 fusion.9
  27.0 0.7 and_select_fusion
  27.7 0.1 add_minimum_fusion
  27.7 0.1 min.6.chosen_ref
  27.8 0.0 copy-start.2
  27.8 1.9 copy-done.2
  29.7 0.0 copy-start.3
  29.7 1.1 copy-done.3
  30.9 0.0 copy-start.4
  30.9 1.1 copy-done.4
  32.0 0.0 copy-start.5
  32.0 0.7 copy-done.5
  32.7 24.5 %shard_map.64.sent_ref = bf16[8,3,128,512]{3,2,1,0:T(8,128)(2,1)S(1)} custom-call(s32[24]{0:T(128)S(1)} %min.6.chosen_ref, bf16[3072,512]{1,0:T(8,128)(2,1)S(1)} %copy-done.2, bf16[3072,128]{1,0:T(8,128)(2,1)S(1)} %copy-done.3, bf16[3072,128]{1,0:T(8,128)(2,1)S(1)} %copy-done.4, s32[24,128]{1,0:T(8,128)S(1)} %bitcast.5), custom_call_target="tpu_custom_call" | custom-call | flops 805306368 | bytes 6291456 | tf_op jit(solution)/shard_map/pallas_call | solution.py:57
  57.2 0.0 copy-start
  57.2 1.7 copy-done
  58.9 0.1 select_reduce_fusion
  59.0 0.1 fusion.3.slots_ref
  59.1 0.0 collective-permute-done.far_weight_ref
  59.1 0.0 copy-start.6
  59.1 0.8 copy-done.6
  59.9 120.3 %shard_map.65 = (bf16[4,8,3,128,512]{4,3,2,1,0:T(8,128)(2,1)}, bf16[8,256,1024]{2,1,0:T(8,128)(2,1)}) custom-call(bf16[8,3,128,512]{3,2,1,0:T(8,128)(2,1)} %copy-done, bf16[256,1024]{1,0:T(8,128)(2,1)} %weight_ref.1, bf16[256,1024]{1,0:T(8,128)(2,1)} %copy-done.6), custom_call_target="tpu_custom_call" | custom-call | bytes 94371840 | tf_op jit(solution)/shard_map/pallas_call | solution.py:221
  180.2 0.0 copy-start.1
  180.2 2.2 %copy-done.1 = bf16[8,256,1024]{2,1,0:T(8,128)(2,1)S(1)} copy-done((bf16[8,256,1024]{2,1,0:T(8,128)(2,1)S(1)}, bf16[8,256,1024]{2,1,0:T(8,128)(2,1)}, u32[]{:S(2)}) %copy-start.1) | copy-done | bytes 4194328
  182.3 17.1 %shard_map.66 = bf16[2816,1024]{1,0:T(8,128)(2,1)} custom-call(s32[22]{0:T(128)S(1)} %fusion.3.slots_ref, bf16[4,24,128,512]{3,2,1,0:T(8,128)(2,1)} %bitcast.6, bf16[4,24,128,512]{3,2,1,0:T(8,128)(2,1)} %bitcast.7, bf16[2048,1024]{1,0:T(8,128)(2,1)S(1)} %bitcast.4), custom_call_target="tpu_custom_call" | custom-call | tf_op jit(solution)/shard_map/pallas_call | solution.py:267
  (4 shorter events, 0.0 us)
Async XLA Ops:
  0.0 59.1 %collective-permute-start = (bf16[256,1024]{1,0:T(8,128)(2,1)}, bf16[256,1024]{1,0:T(8,128)(2,1)S(1)}, u32[]{:S(2)}, u32[]{:S(2)}) collective-permute-start(bf16[256,1024]{1,0:T(8,128)(2,1)} %weight_ref.1), channel_id=1, source_target_pairs={{0,16},{4,20},{8,24},{12,28},{16,0},{20,4},{24,8},{28,12},{1,17},{... | collective-permute-start | bytes 1572872 | tf_op jit(solution)/shard_map/ppermute | solution.py:289
  27.8 1.9 copy-start.2
  29.7 1.1 copy-start.3
  30.9 1.1 copy-start.4
  32.0 0.7 copy-start.5
  57.2 1.7 copy-start
  59.1 0.8 copy-start.6
  180.2 2.2 %copy-start.1 = (bf16[8,256,1024]{2,1,0:T(8,128)(2,1)S(1)}, bf16[8,256,1024]{2,1,0:T(8,128)(2,1)}, u32[]{:S(2)}) copy-start(bf16[8,256,1024]{2,1,0:T(8,128)(2,1)} %get-tuple-element.8) | copy-start | bytes 12582916

commit v2 on v1

--- a/solution.py
+++ b/solution.py
@@ -13,42 +13,50 @@
 NB = 24
 MESH = pl.DeviceIdType.MESH
 MASKED = -1e30
-
-
-def attend_kernel(per_owner, chosen_ref, queries_ref, keys_ref, values_ref, ids_ref, out_ref):
+VMEM = 60 * 1024 * 1024
+
+
+def attend_kernel(per_owner, plan_ref, queries_ref, keys_ref, values_ref, ids_ref, out_ref):
     step = pl.program_id(0)
     repeat = queries_ref.shape[1] // HEAD_SIZE
     factor = math.log2(math.e) / math.sqrt(HEAD_SIZE)
     row_at = lax.broadcasted_iota(jnp.int32, (BLOCK, BLOCK), 0)
     col_at = lax.broadcasted_iota(jnp.int32, (BLOCK, BLOCK), 1)
     causal = col_at <= row_at
+    ones = jnp.ones((BLOCK, HEAD_SIZE), jnp.bfloat16)
     for layer in range(per_owner):
-        block = chosen_ref[step * per_owner + layer]
+        block = plan_ref[0, step * per_owner + layer]
         rows = pl.ds(pl.multiple_of(block * BLOCK, BLOCK), BLOCK)
         along = jnp.broadcast_to(ids_ref[pl.ds(block, 1), :], (BLOCK, BLOCK))
         down = along.T
-        allowed = (along == down) & causal
-        real = down >= 0
+        bias = jnp.where((along == down) & causal, 0.0, MASKED)
+        value = jnp.where(down >= 0, values_ref[rows, :].astype(jnp.float32), 0.0)
+        value = jnp.concatenate([value.astype(jnp.bfloat16), ones], axis=1)
         key = keys_ref[rows, :]
-        value = values_ref[rows, :]
+        query = queries_ref[rows, :]
+        query = jnp.concatenate(
+            [query[:, h * HEAD_SIZE:(h + 1) * HEAD_SIZE] for h in range(repeat)], axis=0
+        )
+        scores = lax.dot_general(
+            query, key, (((1,), (1,)), ((), ())), preferred_element_type=jnp.float32
+        )
+        weights = []
+        for head in range(repeat):
+            part = scores[head * BLOCK:(head + 1) * BLOCK] + bias
+            highest = jnp.max(part, axis=1, keepdims=True)
+            weights.append(jnp.exp2((part - highest) * factor).astype(jnp.bfloat16))
+        summed = jnp.dot(
+            jnp.concatenate(weights, axis=0), value, preferred_element_type=jnp.float32
+        )
+        summed = summed[:, :HEAD_SIZE] / summed[:, HEAD_SIZE:]
         for head in range(repeat):
             columns = slice(head * HEAD_SIZE, (head + 1) * HEAD_SIZE)
-            query = queries_ref[rows, columns]
-            scores = lax.dot_general(
-                query, key, (((1,), (1,)), ((), ())), preferred_element_type=jnp.float32
+            out_ref[0, layer, :, columns] = summed[head * BLOCK:(head + 1) * BLOCK].astype(
+                out_ref.dtype
             )
-            scores = jnp.where(allowed, scores, MASKED)
-            highest = jnp.max(scores, axis=1, keepdims=True)
-            weights = jnp.exp2((scores - highest) * factor)
-            totals = jnp.sum(weights, axis=1, keepdims=True)
-            summed = jnp.dot(
-                weights.astype(jnp.bfloat16), value, preferred_element_type=jnp.float32
-            )
-            summed = jnp.where(real, summed / totals, 0.0)
-            out_ref[0, layer, :, columns] = summed.astype(out_ref.dtype)
-
-
-def attend(chosen, queries, keys, values, ids, members, per_owner):
+
+
+def attend(plan, queries, keys, values, ids, members, per_owner):
     cols = queries.shape[1]
 
     def whole(array):
@@ -63,13 +71,13 @@
             in_specs=[whole(queries), whole(keys), whole(values), whole(ids)],
             out_specs=pl.BlockSpec((1, per_owner, BLOCK, cols), lambda i, c: (i, 0, 0, 0)),
         ),
-        compiler_params=pltpu.CompilerParams(vmem_limit_bytes=40 * 1024 * 1024),
+        compiler_params=pltpu.CompilerParams(vmem_limit_bytes=VMEM),
         cost_estimate=pl.CostEstimate(
             flops=members * per_owner * cols * BLOCK * BLOCK * 4,
             bytes_accessed=4 * queries.size,
             transcendentals=members * per_owner * cols * BLOCK,
         ),
-    )(chosen, queries, keys, values, ids)
+    )(plan, queries, keys, values, ids)
 
 
 def flip(index, mask):
@@ -79,6 +87,73 @@
             index = index + bit - 2 * bit * ((index // bit) % 2)
         bit *= 2
     return index
+
+
+def plan_kernel(members, per_owner, count_ref, plan_ref, table_ref, send_sem, recv_sem):
+    me = lax.axis_index("dp")
+    mine = lax.axis_index("mp")
+    barrier = pltpu.get_barrier_semaphore()
+    for mask in range(1, members):
+        pl.semaphore_signal(
+            barrier, inc=1, device_id=(flip(me, mask), mine), device_id_type=MESH
+        )
+    pl.semaphore_wait(barrier, members - 1)
+    copies = [
+        pltpu.make_async_remote_copy(
+            src_ref=count_ref,
+            dst_ref=table_ref.at[me],
+            send_sem=send_sem.at[mask],
+            recv_sem=recv_sem.at[mask],
+            device_id=(flip(me, mask), mine),
+            device_id_type=MESH,
+        )
+        for mask in range(1, members)
+    ]
+    for copy in copies:
+        copy.start()
+    own_count = count_ref[...]
+    table_ref[me] = own_count
+    for copy in copies:
+        copy.wait()
+    row = lax.broadcasted_iota(jnp.int32, own_count.shape, 0)
+    lane = lax.broadcasted_iota(jnp.int32, own_count.shape, 1)
+    shift = members.bit_length() - 1
+    start = jnp.zeros_like(own_count)
+    first = jnp.zeros_like(own_count)
+    slots = jnp.zeros_like(own_count)
+    wanted = me + lane * members
+    for member in range(members):
+        count = table_ref[member]
+        first = jnp.where(me == member, start, first)
+        within = wanted - start
+        holds = (within >= 0) & (within < count)
+        slots = jnp.where(
+            holds, member * per_owner + lax.shift_right_logical(within, shift), slots
+        )
+        start = start + count
+    owner = jnp.zeros_like(lane)
+    for member in range(1, members):
+        owner = owner + (lane >= member * per_owner).astype(jnp.int32)
+    layer = lane - owner * per_owner
+    turned = (owner - first + members * NB) & (members - 1)
+    chosen = jnp.minimum(turned + layer * members, NB - 1)
+    chosen = jnp.maximum(chosen, 0)
+    plan_ref[...] = jnp.where(row == 0, chosen, slots)
+
+
+def make_plan(live_counts, members, per_owner):
+    count = jnp.broadcast_to(live_counts[:, None], (8, 128))
+    dma = pltpu.SemaphoreType.DMA
+    return pl.pallas_call(
+        functools.partial(plan_kernel, members, per_owner),
+        out_shape=jax.ShapeDtypeStruct(count.shape, jnp.int32),
+        in_specs=[pl.BlockSpec(memory_space=pltpu.VMEM)],
+        out_specs=pl.BlockSpec(memory_space=pltpu.VMEM),
+        scratch_shapes=[
+            pltpu.VMEM((members,) + count.shape, jnp.int32), dma((members,)), dma((members,))
+        ],
+        compiler_params=pltpu.CompilerParams(collective_id=1, has_side_effects=True),
+    )(count)
 
 
 def exchange_kernel(
@@ -235,7 +310,7 @@
             dma((members,)),
             dma((members,)),
         ],
-        compiler_params=pltpu.CompilerParams(collective_id=0, has_side_effects=True),
+        compiler_params=pltpu.CompilerParams(collective_id=0, has_side_effects=True, vmem_limit_bytes=VMEM),
         cost_estimate=pl.CostEstimate(
             flops=0, bytes_accessed=60 * sent.size, transcendentals=0
         ),
@@ -261,7 +336,7 @@
 
     def picked(which):
         return pl.BlockSpec(
-            (columns, 1, BLOCK, depth), lambda i, s: (0, s[2 * i + which], 0, 0)
+            (columns, 1, BLOCK, depth), lambda i, s: (0, s[1, 2 * i + which], 0, 0)
         )
 
     return pl.pallas_call(
@@ -277,40 +352,26 @@
             ],
             out_specs=pl.BlockSpec((2 * BLOCK, width), lambda i, s: (i, 0)),
         ),
-        compiler_params=pltpu.CompilerParams(vmem_limit_bytes=40 * 1024 * 1024),
+        compiler_params=pltpu.CompilerParams(vmem_limit_bytes=VMEM),
     )(slots, held, held, weight)
 
 
 def body(members, columns, queries, keys, values, doc_ids, live_counts, out_weight):
     per_owner = (NB + members - 1) // members
     kept = NB * 11 // 12
-    own = lax.axis_index("dp")
     half = members // 2
+    plan = make_plan(live_counts, members, per_owner)
+    plan, near_weight = lax.optimization_barrier((plan, out_weight))
     far_weight = lax.ppermute(
-        out_weight, "dp", [(i, (i + half) % members) for i in range(members)]
-    )
-    table = lax.all_gather(live_counts, "dp", axis=0, tiled=True)
-    places = jnp.arange(members, dtype=jnp.int32)
-    before = places[None, :] < places[:, None]
-    starts = jnp.sum(jnp.where(before, table[None, :], 0), axis=1)
-    first_label = jnp.sum(jnp.where(places < own, table, 0))
-    owners = jnp.arange(members, dtype=jnp.int32)[:, None]
-    layers = jnp.arange(per_owner, dtype=jnp.int32)[None, :]
-    chosen = ((owners - first_label) % members + layers * members).reshape(-1)
-    chosen = jnp.minimum(chosen, NB - 1)
-    wanted = own + jnp.arange(kept, dtype=jnp.int32) * members
-    within = wanted[:, None] - starts[None, :]
-    holds = (within >= 0) & (within < table[None, :])
-    slots = jnp.sum(
-        jnp.where(holds, places[None, :] * per_owner + within // members, 0), axis=1
+        near_weight, "dp", [(i, (i + half) % members) for i in range(members)]
     )
     sent = attend(
-        chosen, queries, keys, values, doc_ids.reshape(NB, BLOCK), members, per_owner
+        plan, queries, keys, values, doc_ids.reshape(NB, BLOCK), members, per_owner
     )
     held, full = exchange(sent, out_weight, far_weight, members, columns)
     held = held.reshape(columns, members * per_owner, BLOCK, queries.shape[1])
     full = full.reshape(members * out_weight.shape[0], out_weight.shape[1])
-    return project(slots, held, full, kept)
+    return project(plan, held, full, kept)
 
 
 def solution(mesh):

time: 200 us -> 175 us (0.88)
  blocking collectives: 20.6 us -> 0 us
  waiting for transfers between devices: 0.01 us -> 11.8 us
  local copies, waits for them, and re-layouts: 11.6 us -> 1.39 us
  Pallas kernels: 162 us -> 158 us
    unnamed x1 -> x0, blocking collectives: 20.6 us -> none
    pallas_call x1, Pallas kernels: 24.5 us -> 11.7 us  [attend(): pl.pallas_call(functools.partial(attend_kernel, per_owner), out_shape=jax...]
    ppermute x1, waiting for transfers between devices: 0.01 us -> 11.8 us  [body(): lax.ppermute(near_weight, 'dp', [(i, (i + half) % members) for i in range...]
    unnamed x17 -> x2, local copies, waits for them, and re-layouts: 11.5 us -> 0.79 us
    pallas_call x0 -> x1, Pallas kernels: none -> 8.22 us  [make_plan(): pl.pallas_call(functools.partial(plan_kernel, members, per_owner), out_sh...]
  transfers between devices with their start and end apart: 1 -> 1, of which waited for: 0 -> 1; matrix products, arithmetic and copies ran while one was open for 2% -> 0% of each run, Pallas kernels for 12% -> 7%
where the time goes in v2:
time: 175 us; the launch traced here: 174 us
  Pallas kernels  158 us (90%)
  waiting for transfers between devices  11.8 us (7%)
  starting transfers between devices  1.89 us (1%)
    pallas_call x1, Pallas kernels, exchange(): pl.pallas_call(functools.partial(exchange_kernel, members, columns, per_o...  120 us
    pallas_call x1, Pallas kernels, project(): pl.pallas_call(functools.partial(project_kernel, columns), out_shape=jax....  18.6 us
    ppermute x1, waiting for transfers between devices, body(): lax.ppermute(near_weight, 'dp', [(i, (i + half) % members) for i in range...  11.8 us
    pallas_call x1, Pallas kernels, attend(): pl.pallas_call(functools.partial(attend_kernel, per_owner), out_shape=jax...  11.7 us
    pallas_call x1, Pallas kernels, make_plan(): pl.pallas_call(functools.partial(plan_kernel, members, per_owner), out_sh...  8.22 us
  transfers between devices with their start and end apart: 1, of which 1 were waited for; matrix products, arithmetic and copies ran while one was open for 0% of the time, Pallas kernels for 7%

profile of v2, /device:TPU:1, one launch (start us, length us, event | category | flops | bytes accessed | tf_op | source)
XLA Modules:
  0.0 174.1 jit_solution(17485922515738869125)
XLA Ops:
  0.7 0.6 broadcast_in_dim.9.count_ref
  1.2 8.2 %shard_map.64.plan_ref.slots_ref = s32[8,128]{1,0:T(8,128)} custom-call(s32[8,128]{1,0:T(8,128)} %broadcast_in_dim.9.count_ref), custom_call_target="tpu_custom_call" | custom-call | tf_op jit(solution)/shard_map/pallas_call | solution.py:147
  9.5 1.9 %collective-permute-start = (bf16[256,1024]{1,0:T(8,128)(2,1)}, bf16[256,1024]{1,0:T(8,128)(2,1)S(1)}, u32[]{:S(2)}, u32[]{:S(2)}) collective-permute-start(bf16[256,1024]{1,0:T(8,128)(2,1)} %weight_ref.1), channel_id=1, source_target_pairs={{0,16},{4,20},{8,24},{12,28},{16,0},{20,4},{24,8},{28,12},{1,17},{... | collective-permute-start | bytes 1572872 | tf_op jit(solution)/shard_map/ppermute | solution.py:365
  11.4 11.7 %shard_map.65.sent_ref = bf16[8,3,128,512]{3,2,1,0:T(8,128)(2,1)} custom-call(s32[8,128]{1,0:T(8,128)} %shard_map.64.plan_ref.slots_ref, bf16[3072,512]{1,0:T(8,128)(2,1)} %queries_ref.1, bf16[3072,128]{1,0:T(8,128)(2,1)} %keys_ref.1, bf16[3072,128]{1,0:T(8,128)(2,1)} %values_ref.1, s32[24,128]{1,0:T(8,128)} %bitcast.8), custom_call_target="tpu_custom_call" | custom-call | flops 805306368 | bytes 6291456 | tf_op jit(solution)/shard_map/pallas_call | solution.py:65
  23.1 11.8 %collective-permute-done.far_weight_ref = bf16[256,1024]{1,0:T(8,128)(2,1)S(1)} collective-permute-done((bf16[256,1024]{1,0:T(8,128)(2,1)}, bf16[256,1024]{1,0:T(8,128)(2,1)S(1)}, u32[]{:S(2)}, u32[]{:S(2)}) %collective-permute-start) | collective-permute-done | bytes 524320 | tf_op jit(solution)/shard_map/ppermute | solution.py:365
  34.9 0.0 copy-start
  34.9 0.8 copy-done
  35.7 119.8 %shard_map.66 = (bf16[4,8,3,128,512]{4,3,2,1,0:T(8,128)(2,1)}, bf16[8,256,1024]{2,1,0:T(8,128)(2,1)}) custom-call(bf16[8,3,128,512]{3,2,1,0:T(8,128)(2,1)} %shard_map.65.sent_ref, bf16[256,1024]{1,0:T(8,128)(2,1)} %weight_ref.1, bf16[256,1024]{1,0:T(8,128)(2,1)} %copy-done), custom_call_target="tpu_custom_call" | custom-call | bytes 94371840 | tf_op jit(solution)/shard_map/pallas_call | solution.py:296
  155.4 18.6 %shard_map.67 = bf16[2816,1024]{1,0:T(8,128)(2,1)} custom-call(s32[8,128]{1,0:T(8,128)} %shard_map.64.plan_ref.slots_ref, bf16[4,24,128,512]{3,2,1,0:T(8,128)(2,1)} %bitcast.5, bf16[4,24,128,512]{3,2,1,0:T(8,128)(2,1)} %bitcast.6, bf16[2048,1024]{1,0:T(8,128)(2,1)} %bitcast.7), custom_call_target="tpu_custom_call" | custom-call | tf_op jit(solution)/shard_map/pallas_call | solution.py:342
Async XLA Ops:
  9.5 25.4 %collective-permute-start = (bf16[256,1024]{1,0:T(8,128)(2,1)}, bf16[256,1024]{1,0:T(8,128)(2,1)S(1)}, u32[]{:S(2)}, u32[]{:S(2)}) collective-permute-start(bf16[256,1024]{1,0:T(8,128)(2,1)} %weight_ref.1), channel_id=1, source_target_pairs={{0,16},{4,20},{8,24},{12,28},{16,0},{20,4},{24,8},{28,12},{1,17},{... | collective-permute-start | bytes 1572872 | tf_op jit(solution)/shard_map/ppermute | solution.py:365
  34.9 0.8 copy-start

commit v3 on v2

--- a/solution.py
+++ b/solution.py
@@ -245,12 +245,13 @@
                 start(mp_copy(place, bit, mask, layer))
 
     order = sorted(range(1, members), key=lambda t: (-(bin(t).count("1") % 2), t))
-    spread_weight(0, top)
-    spread_weight(top, top)
     for layer in range(per_owner):
         spread(0, columns, 0, layer)
         for mask in order:
             start(dp_copy(mask, layer, me))
+        if layer == 0:
+            spread_weight(0, top)
+            spread_weight(top, top)
     for copy in local:
         copy.start()
 
@@ -272,7 +273,7 @@
             if mask:
                 dp_copy(mask, layer, me).wait_recv()
                 spread(0, columns, mask, layer)
-        if at % 3 == 2 and weights:
+        if at >= members and at % 2 and weights:
             arrived = weights.pop(0)
             lowest = arrived & -arrived
             weight_copy(arrived ^ lowest, lowest).wait_recv()

time: 175 us -> 163 us (0.931)
  Pallas kernels: 158 us -> 147 us
    pallas_call x1, Pallas kernels: 120 us -> 109 us  [exchange(): pl.pallas_call(functools.partial(exchange_kernel, members, columns, per_o...]
where the time goes in v3:
time: 163 us
  Pallas kernels  147 us (90%)
  waiting for transfers between devices  11.8 us (7%)
  starting transfers between devices  1.89 us (1%)
    pallas_call x1, Pallas kernels, exchange(): pl.pallas_call(functools.partial(exchange_kernel, members, columns, per_o...  109 us
    pallas_call x1, Pallas kernels, project(): pl.pallas_call(functools.partial(project_kernel, columns), out_shape=jax....  18.6 us
    ppermute x1, waiting for transfers between devices, body(): lax.ppermute(near_weight, 'dp', [(i, (i + half) % members) for i in range...  11.8 us
    pallas_call x1, Pallas kernels, attend(): pl.pallas_call(functools.partial(attend_kernel, per_owner), out_shape=jax...  11.7 us
    pallas_call x1, Pallas kernels, make_plan(): pl.pallas_call(functools.partial(plan_kernel, members, per_owner), out_sh...  8.22 us
  transfers between devices with their start and end apart: 1, of which 1 were waited for; matrix products, arithmetic and copies ran while one was open for 0% of the time, Pallas kernels for 7%

profile of v3, /device:TPU:1, one launch (start us, length us, event | category | flops | bytes accessed | tf_op | source)
XLA Modules:
  0.0 162.9 jit_solution(1702861943187163192)
XLA Ops:
  0.7 0.6 broadcast_in_dim.9.count_ref
  1.2 8.2 %shard_map.64.plan_ref.slots_ref = s32[8,128]{1,0:T(8,128)} custom-call(s32[8,128]{1,0:T(8,128)} %broadcast_in_dim.9.count_ref), custom_call_target="tpu_custom_call" | custom-call | tf_op jit(solution)/shard_map/pallas_call | solution.py:147
  9.5 1.9 %collective-permute-start = (bf16[256,1024]{1,0:T(8,128)(2,1)}, bf16[256,1024]{1,0:T(8,128)(2,1)S(1)}, u32[]{:S(2)}, u32[]{:S(2)}) collective-permute-start(bf16[256,1024]{1,0:T(8,128)(2,1)} %weight_ref.1), channel_id=1, source_target_pairs={{0,16},{4,20},{8,24},{12,28},{16,0},{20,4},{24,8},{28,12},{1,17},{... | collective-permute-start | bytes 1572872 | tf_op jit(solution)/shard_map/ppermute | solution.py:366
  11.4 11.7 %shard_map.65.sent_ref = bf16[8,3,128,512]{3,2,1,0:T(8,128)(2,1)} custom-call(s32[8,128]{1,0:T(8,128)} %shard_map.64.plan_ref.slots_ref, bf16[3072,512]{1,0:T(8,128)(2,1)} %queries_ref.1, bf16[3072,128]{1,0:T(8,128)(2,1)} %keys_ref.1, bf16[3072,128]{1,0:T(8,128)(2,1)} %values_ref.1, s32[24,128]{1,0:T(8,128)} %bitcast.8), custom_call_target="tpu_custom_call" | custom-call | flops 805306368 | bytes 6291456 | tf_op jit(solution)/shard_map/pallas_call | solution.py:65
  23.1 11.8 %collective-permute-done.far_weight_ref = bf16[256,1024]{1,0:T(8,128)(2,1)S(1)} collective-permute-done((bf16[256,1024]{1,0:T(8,128)(2,1)}, bf16[256,1024]{1,0:T(8,128)(2,1)S(1)}, u32[]{:S(2)}, u32[]{:S(2)}) %collective-permute-start) | collective-permute-done | bytes 524320 | tf_op jit(solution)/shard_map/ppermute | solution.py:366
  34.9 0.0 copy-start
  34.9 0.8 copy-done
  35.7 108.5 %shard_map.66 = (bf16[4,8,3,128,512]{4,3,2,1,0:T(8,128)(2,1)}, bf16[8,256,1024]{2,1,0:T(8,128)(2,1)}) custom-call(bf16[8,3,128,512]{3,2,1,0:T(8,128)(2,1)} %shard_map.65.sent_ref, bf16[256,1024]{1,0:T(8,128)(2,1)} %weight_ref.1, bf16[256,1024]{1,0:T(8,128)(2,1)} %copy-done), custom_call_target="tpu_custom_call" | custom-call | bytes 94371840 | tf_op jit(solution)/shard_map/pallas_call | solution.py:297
  144.2 18.6 %shard_map.67 = bf16[2816,1024]{1,0:T(8,128)(2,1)} custom-call(s32[8,128]{1,0:T(8,128)} %shard_map.64.plan_ref.slots_ref, bf16[4,24,128,512]{3,2,1,0:T(8,128)(2,1)} %bitcast.5, bf16[4,24,128,512]{3,2,1,0:T(8,128)(2,1)} %bitcast.6, bf16[2048,1024]{1,0:T(8,128)(2,1)} %bitcast.7), custom_call_target="tpu_custom_call" | custom-call | tf_op jit(solution)/shard_map/pallas_call | solution.py:343
Async XLA Ops:
  9.5 25.4 %collective-permute-start = (bf16[256,1024]{1,0:T(8,128)(2,1)}, bf16[256,1024]{1,0:T(8,128)(2,1)S(1)}, u32[]{:S(2)}, u32[]{:S(2)}) collective-permute-start(bf16[256,1024]{1,0:T(8,128)(2,1)} %weight_ref.1), channel_id=1, source_target_pairs={{0,16},{4,20},{8,24},{12,28},{16,0},{20,4},{24,8},{28,12},{1,17},{... | collective-permute-start | bytes 1572872 | tf_op jit(solution)/shard_map/ppermute | solution.py:366
  34.9 0.8 copy-start
